TPU v7x, 32 devices: a whole 2x2x4 slice. The times are simulated.
32 devices in a mesh: grp: 2 (over y), seq: 16 (over z, x, core), head: 1.
Axes of the slice: x: 2, y: 2, z: 4, core: 2. Of those that a mesh axis runs over, the one named last changes fastest.
Arguments:
- queries: bfloat16 [2048, 1, 128], P(('grp', 'seq'), 'head'), parts along dimension 0, may hold values from -6 to 6
- keys: bfloat16 [256, 512, 8, 128], P(('grp', 'seq'), None, 'head'), parts along dimension 0, may hold values from -28 to 28
- values: bfloat16 [256, 512, 8, 128], P(('grp', 'seq'), None, 'head'), parts along dimension 0, may hold values from -6 to 6
- lengths: int32 [32], P('grp'), parts along dimension 0, may hold values from 1 to 4096, 40960 in all
- slot_block: int32 [256], P(('grp', 'seq')), parts along dimension 0, may hold values from 0 to 127, each once
Outputs:
- attended: bfloat16 [2048, 1, 128], P(('grp', 'seq'), 'head'), parts along dimension 0
There are 2 independent parts, one for each index of `grp`. A program takes and returns all parts, laid end to end along the dimension named above; each array names one. Nothing has to cross between parts.
Inputs may be any that keep to these rules, and one draw needn't show every extreme that they name: `slot_block`: each slot holds a different logical block; every block of every sequence has a slot. `lengths`: every sequence has at least one token.
All inputs are finite; a program needn't handle non-finite values.
Results may differ from a plain program's by a relative error of at most 0.0055.
Values may be sent and summed in bfloat16 or wider, within the bound.
A program may use at most 64 MiB of HBM per device.

v0:
```python
import jax
import jax.numpy as jnp
from jax import lax
from jax.sharding import PartitionSpec as P


def slot_partial(q_one, key_one, val_one, live_one, factor):
    scores = jnp.einsum("kgd,tkd->kgt", q_one, key_one, preferred_element_type=jnp.float32) * factor
    live_row = live_one[None, None, :]
    peak = jnp.max(jnp.where(live_row, scores, -1e30), axis=-1)
    weights = jnp.where(live_row, jnp.exp(scores - peak[..., None]), 0.0).astype(jnp.bfloat16)
    total = jnp.sum(weights.astype(jnp.float32), axis=-1)
    partial_out = jnp.einsum("kgt,tkd->kgd", weights, val_one, preferred_element_type=jnp.float32)
    return (peak, total, partial_out)


def body(queries, keys, values, lengths, slot_block):
    rows = lax.all_gather(queries, "seq", axis=0, tiled=True)
    slots, block, kv_local, head_dim = keys.shape
    batch = lengths.shape[0]
    group = rows.shape[0] // batch // kv_local
    factor = head_dim ** (-0.5)
    q_grouped = rows.reshape(batch, kv_local, group, head_dim)
    per_seq = slots * lax.axis_size("seq") // batch
    seq_of = slot_block // per_seq
    blk_of = slot_block % per_seq
    q_slot = jnp.take(q_grouped, seq_of, axis=0)
    positions = blk_of[:, None] * block + jnp.arange(block, dtype=jnp.int32)[None, :]
    live = positions < jnp.take(lengths, seq_of)[:, None]

    def run_slot(q_one, key_one, val_one, live_one):
        return slot_partial(q_one, key_one, val_one, live_one, factor)

    peaks, totals, partials = jax.vmap(run_slot)(q_slot, keys, values, live)
    member = seq_of[:, None] == jnp.arange(batch, dtype=jnp.int32)[None, :]
    best = jnp.max(jnp.where(member[:, :, None, None], peaks[:, None], -1e30), axis=0)
    scaled = jnp.exp(peaks - jnp.take(best, seq_of, axis=0))
    onehot = member.astype(jnp.float32)
    denom = jnp.einsum("sb,skg->bkg", onehot, scaled * totals, precision=lax.Precision.HIGHEST)
    numer = jnp.einsum(
        "sb,skgd->bkgd", onehot, scaled[..., None] * partials, precision=lax.Precision.HIGHEST
    )
    row_count = rows.shape[0]
    share = row_count // lax.axis_size("seq")
    top_peak = lax.pmax(best, "seq")
    rescale = jnp.exp(best - top_peak)
    own_total, own_out = (
        lax.psum_scatter(
            (denom * rescale).reshape(row_count), "seq", scatter_dimension=0, tiled=True
        ),
        lax.psum_scatter(
            (numer * rescale[..., None]).reshape(row_count, head_dim),
            "seq",
            scatter_dimension=0,
            tiled=True,
        ),
    )
    result = own_out / own_total[:, None]
    return result.astype(jnp.bfloat16).reshape(share, 1, head_dim)


def solution(mesh):
    placed = (
        P(("grp", "seq"), "head", None),
        P(("grp", "seq"), None, "head", None),
        P(("grp", "seq"), None, "head", None),
        P("grp"),
        P(("grp", "seq")),
    )
    return jax.shard_map(
        body, mesh=mesh, in_specs=placed, out_specs=P(("grp", "seq"), "head", None), check_vma=False
    )
```

profile of v0, /device:TPU:0, one launch (start us, length us, event | category | flops | bytes accessed | tf_op | source)
XLA Modules:
  0.0 166.0 jit_solution(9803594081013029989)
XLA Ops:
  6.5 0.0 copy-start
  6.5 0.0 reduce-scatter.2.cloned.1.call-start
  6.5 0.7 compare_select_fusion
  7.2 0.1 iota_compare_fusion
  7.3 0.0 copy-done
  7.3 0.6 gather_fusion
  8.0 24.1 %all_gather.3 = bf16[1024,1,128]{2,0,1:T(8,128)(2,1)S(1)} all-gather(bf16[64,1,128]{2,0,1:T(8,128)(2,1)} %param.5), channel_id=1, replica_groups=mesh['grp'=2,'seq'=16,'head'=1] {'seq'}, dimensions={0}, use_global_device_ids=true | all-gather | bytes 278528 | tf_op jit(solution)/shard_map/all_gather | solution.py:18
  32.0 0.6 gather_fusion.1
  32.6 0.1 add_compare_fusion
  32.7 5.8 %select_reduce_fusion = (f32[8,8,8]{2,1,0:T(8,128)S(1)}, f32[8,8,8,512]{3,2,1,0:T(8,128)S(1)}) fusion(pred[8,512]{1,0:T(8,128)(4,1)S(1)} %add_compare_fusion, bf16[8,512,8,128]{3,2,1,0:T(8,128)(2,1)} %param.6, bf16[8,8,8,128]{3,2,1,0:T(8,128)(2,1)S(1)} %gather_fusion.1, pred[8]{0:T(512)(128)(4,1)S(1)} %get-tuple-element.8), kind=kOutput, calls=%fused_computation.14 | convolution fusion | flops 67960320 | bytes 9574408 | tf_op jit(solution)/shard_map/vmap(kgd,tkd->kgt)/dot_general | solution.py:8
  38.4 0.0 copy-start.1
  38.4 0.1 select_reduce_fusion.1
  38.6 57.8 %pmax.7 = f32[16,8,8]{0,2,1:T(8,128)S(1)} all-reduce(f32[16,8,8]{0,2,1:T(8,128)S(1)} %select_reduce_fusion.1), channel_id=1, replica_groups=mesh['grp'=2,'seq'=16,'head'=1] {'seq'}, use_global_device_ids=true, to_apply=%region_2.3 | all-reduce | flops 1024 | bytes 8192 | tf_op jit(solution)/shard_map/pmax | solution.py:45
  96.4 0.1 copy.23
  96.6 0.3 convert_reduce_fusion
  96.9 0.6 gather_fusion.2
  97.5 0.1 fusion.23
  97.6 5.0 %fusion.7 = f32[8,8,8,128]{3,2,1,0:T(8,128)S(1)} fusion(bf16[8,512,8,128]{3,2,1,0:T(8,128)(2,1)} %param.7, f32[8,8,8]{2,1,0:T(8,128)S(1)} %get-tuple-element.6, f32[8,8,8,512]{3,2,1,0:T(8,128)S(1)} %get-tuple-element.13, f32[8,8,8]{2,1,0:T(8,128)S(1)} %get-tuple-element.12, pred[8,512]{1,0:T(8,128)(4,1)S(1)} %add_compare_fusion), kind=kOutput, calls=%fused_computation.9 | convolution fusion | flops 67960832 | bytes 9707520 | tf_op jit(solution)/shard_map/vmap(kgt,tkd->kgd)/dot_general | solution.py:13
  102.5 0.6 convolution_multiply_fusion
  103.1 1.0 copy.26
  104.0 0.0 reduce-scatter.2.cloned.1.call-update
  104.1 0.1 copy.27
  104.2 0.2 fusion.10
  104.4 0.1 copy.28
  104.5 0.1 reshape.84
  104.6 0.0 copy-done.1
  104.6 0.6 dynamic-slice
  105.8 29.6 %all-reduce = f32[1024]{0:T(1024)S(1)} all-reduce(f32[1024]{0:T(1024)S(1)} %reshape.84), channel_id=3, replica_groups=mesh['grp'=2,'seq'=16,'head'=1] {'seq'}, use_global_device_ids=true, to_apply=%region_5.6.clone | all-reduce | flops 1024 | bytes 8192
  135.4 0.1 dynamic-slice.1
  135.5 22.2 %reduce-scatter.2.cloned.1.call-done = f32[64,128]{1,0:T(8,128)} async-done(((f32[1024,128]{1,0:T(8,128)}), f32[64,128]{1,0:T(8,128)}) %reduce-scatter.2.cloned.1.call-update) | async-done | bytes 32784 | tf_op jit(solution)/shard_map/reduce_scatter | solution.py:51
  157.7 1.4 fusion.16
  (3 shorter events, 0.0 us)
Async XLA Ops:
  6.5 0.8 copy-start
  6.5 151.2 %reduce-scatter.2.cloned.1.call-start = ((), (), s32[]{:S(2)}) async-start(), calls=%async_computation.1 | async-start | bytes 557056 | tf_op jit(solution)/shard_map/reduce_scatter | solution.py:51
  38.4 66.1 %copy-start.1 = (u32[32]{0:T(128)S(1)}, u32[32]{0:T(128)}, u32[]{:S(2)}) copy-start(u32[32]{0:T(128)} %constant.84) | copy-start | bytes 388
Sparse Core Ops, SparseCore 0:
  104.2 53.4 reduce-scatter.1
where the time goes:
time: 166 us
  blocking collectives  111 us (67%)
  waiting for transfers between devices  22.2 us (13%)
  between operations  14.1 us (8%)
  matrix products  11.5 us (7%)
  local copies, waits for them, and re-layouts  3.73 us (2%)
  other arithmetic  2.89 us (2%)
    pmax x1, blocking collectives, body(): top_peak = lax.pmax(best, 'seq')  57.8 us
    unnamed x1, blocking collectives  29.6 us
    all_gather x1, blocking collectives, body(): rows = lax.all_gather(queries, 'seq', axis=0, tiled=True)  24.1 us
    reduce_scatter x1, waiting for transfers between devices, body(): lax.psum_scatter((numer * rescale[..., None]).reshape(row_count, head_dim...  22.2 us
    dot_general x1, matrix products, slot_partial(): jnp.einsum('kgd,tkd->kgt', q_one, key_one, preferred_element_type=jnp.flo...  5.79 us
    dot_general x1, matrix products, slot_partial(): jnp.einsum('kgt,tkd->kgd', weights, val_one, preferred_element_type=jnp.f...  4.96 us
  transfers between devices with their start and end apart: 1, of which 1 were waited for; matrix products, arithmetic and copies ran while one was open for 1% of the time, Pallas kernels for 0%

commit v1 on v0

--- a/solution.py
+++ b/solution.py
@@ -2,6 +2,19 @@
 import jax.numpy as jnp
 from jax import lax
 from jax.sharding import PartitionSpec as P
+
+
+def part_stops_all_all(patch):
+    degree = lax.axis_size("seq")
+    found = [(i, (i + 1) % degree) for i in range(degree)]
+    w2 = [None] * degree
+    w2[degree - 1] = patch
+    for dd in range(degree - 2, -1, -1):
+        w2[dd] = lax.ppermute(w2[dd + 1], "seq", found)
+    everything = jnp.concatenate(w2, axis=0)
+    current_arr = lax.axis_index("seq")
+    local_out = (current_arr + 1) * patch.shape[0]
+    return jnp.roll(everything, shift=local_out, axis=0)
 
 
 def slot_partial(q_one, key_one, val_one, live_one, factor):
@@ -15,7 +28,7 @@
 
 
 def body(queries, keys, values, lengths, slot_block):
-    rows = lax.all_gather(queries, "seq", axis=0, tiled=True)
+    rows = part_stops_all_all(queries)
     slots, block, kv_local, head_dim = keys.shape
     batch = lengths.shape[0]
     group = rows.shape[0] // batch // kv_local

time: 166 us -> 232 us (1.40)
  waiting for transfers between devices: 22.2 us -> 110 us
  blocking collectives: 111 us -> 87.2 us
    ppermute x0 -> x15, waiting for transfers between devices: none -> 87.1 us  [part_stops_all_all(): w2[dd] = lax.ppermute(w2[dd + 1], 'seq', found)]
    all_gather x1 -> x0, blocking collectives: 24.1 us -> none  [body(): rows = lax.all_gather(queries, 'seq', axis=0, tiled=True)]
  transfers between devices with their start and end apart: 1 -> 16, of which waited for: 1 -> 16; matrix products, arithmetic and copies ran while one was open for 1% -> 1% of each run, Pallas kernels for 0% -> 0%
where the time goes in v1:
time: 232 us
  waiting for transfers between devices  110 us (47%)
  blocking collectives  87.2 us (38%)
  between operations  14.3 us (6%)
  matrix products  11.5 us (5%)
  local copies, waits for them, and re-layouts  5.47 us (2%)
  other arithmetic  2.87 us (1%)
    ppermute x15, waiting for transfers between devices, part_stops_all_all(): w2[dd] = lax.ppermute(w2[dd + 1], 'seq', found)  87.1 us
    pmax x1, blocking collectives, body(): top_peak = lax.pmax(best, 'seq')  57.6 us
    unnamed x1, blocking collectives  29.6 us
    reduce_scatter x1, waiting for transfers between devices, body(): lax.psum_scatter((numer * rescale[..., None]).reshape(row_count, head_dim...  22.7 us
    dot_general x1, matrix products, slot_partial(): jnp.einsum('kgd,tkd->kgt', q_one, key_one, preferred_element_type=jnp.flo...  5.79 us
    dot_general x1, matrix products, slot_partial(): jnp.einsum('kgt,tkd->kgd', weights, val_one, preferred_element_type=jnp.f...  4.97 us
  transfers between devices with their start and end apart: 16, of which 16 were waited for; matrix products, arithmetic and copies ran while one was open for 1% of the time, Pallas kernels for 0%

profile of v1, /device:TPU:0, one launch (start us, length us, event | category | flops | bytes accessed | tf_op | source)
XLA Modules:
  0.0 231.7 jit_solution(11302746372268074752)
XLA Ops:
  6.5 0.5 collective-permute-start
  7.0 6.6 %collective-permute-done = bf16[64,1,128]{2,0,1:T(8,128)(2,1)S(1)} collective-permute-done((bf16[64,1,128]{2,0,1:T(8,128)(2,1)}, bf16[64,1,128]{2,0,1:T(8,128)(2,1)S(1)}, u32[]{:S(2)}, u32[]{:S(2)}) %collective-permute-start) | collective-permute-done | bytes 16416 | tf_op jit(solution)/shard_map/ppermute | solution.py:13
  13.6 0.0 collective-permute-start.1
  13.6 5.9 %collective-permute-done.1 = bf16[64,1,128]{2,0,1:T(8,128)(2,1)S(1)} collective-permute-done((bf16[64,1,128]{2,0,1:T(8,128)(2,1)S(1)}, bf16[64,1,128]{2,0,1:T(8,128)(2,1)S(1)}, u32[]{:S(2)}, u32[]{:S(2)}) %collective-permute-start.1) | collective-permute-done | bytes 16416 | tf_op jit(solution)/shard_map/ppermute | solution.py:13
  19.5 5.9 %collective-permute-done.2 = bf16[64,1,128]{2,0,1:T(8,128)(2,1)S(1)} collective-permute-done((bf16[64,1,128]{2,0,1:T(8,128)(2,1)S(1)}, bf16[64,1,128]{2,0,1:T(8,128)(2,1)S(1)}, u32[]{:S(2)}, u32[]{:S(2)}) %collective-permute-start.2) | collective-permute-done | bytes 16416 | tf_op jit(solution)/shard_map/ppermute | solution.py:13
  25.3 5.9 %collective-permute-done.3 = bf16[64,1,128]{2,0,1:T(8,128)(2,1)S(1)} collective-permute-done((bf16[64,1,128]{2,0,1:T(8,128)(2,1)S(1)}, bf16[64,1,128]{2,0,1:T(8,128)(2,1)S(1)}, u32[]{:S(2)}, u32[]{:S(2)}) %collective-permute-start.3) | collective-permute-done | bytes 16416 | tf_op jit(solution)/shard_map/ppermute | solution.py:13
  31.2 5.9 %collective-permute-done.4 = bf16[64,1,128]{2,0,1:T(8,128)(2,1)S(1)} collective-permute-done((bf16[64,1,128]{2,0,1:T(8,128)(2,1)S(1)}, bf16[64,1,128]{2,0,1:T(8,128)(2,1)S(1)}, u32[]{:S(2)}, u32[]{:S(2)}) %collective-permute-start.4) | collective-permute-done | bytes 16416 | tf_op jit(solution)/shard_map/ppermute | solution.py:13
  37.1 5.9 %collective-permute-done.5 = bf16[64,1,128]{2,0,1:T(8,128)(2,1)S(1)} collective-permute-done((bf16[64,1,128]{2,0,1:T(8,128)(2,1)S(1)}, bf16[64,1,128]{2,0,1:T(8,128)(2,1)S(1)}, u32[]{:S(2)}, u32[]{:S(2)}) %collective-permute-start.5) | collective-permute-done | bytes 16416 | tf_op jit(solution)/shard_map/ppermute | solution.py:13
  42.9 5.9 %collective-permute-done.6 = bf16[64,1,128]{2,0,1:T(8,128)(2,1)S(1)} collective-permute-done((bf16[64,1,128]{2,0,1:T(8,128)(2,1)S(1)}, bf16[64,1,128]{2,0,1:T(8,128)(2,1)S(1)}, u32[]{:S(2)}, u32[]{:S(2)}) %collective-permute-start.6) | collective-permute-done | bytes 16416 | tf_op jit(solution)/shard_map/ppermute | solution.py:13
  48.8 5.9 %collective-permute-done.7 = bf16[64,1,128]{2,0,1:T(8,128)(2,1)S(1)} collective-permute-done((bf16[64,1,128]{2,0,1:T(8,128)(2,1)S(1)}, bf16[64,1,128]{2,0,1:T(8,128)(2,1)S(1)}, u32[]{:S(2)}, u32[]{:S(2)}) %collective-permute-start.7) | collective-permute-done | bytes 16416 | tf_op jit(solution)/shard_map/ppermute | solution.py:13
  54.7 5.9 %collective-permute-done.8 = bf16[64,1,128]{2,0,1:T(8,128)(2,1)S(1)} collective-permute-done((bf16[64,1,128]{2,0,1:T(8,128)(2,1)S(1)}, bf16[64,1,128]{2,0,1:T(8,128)(2,1)S(1)}, u32[]{:S(2)}, u32[]{:S(2)}) %collective-permute-start.8) | collective-permute-done | bytes 16416 | tf_op jit(solution)/shard_map/ppermute | solution.py:13
  60.5 5.9 %collective-permute-done.9 = bf16[64,1,128]{2,0,1:T(8,128)(2,1)S(1)} collective-permute-done((bf16[64,1,128]{2,0,1:T(8,128)(2,1)S(1)}, bf16[64,1,128]{2,0,1:T(8,128)(2,1)S(1)}, u32[]{:S(2)}, u32[]{:S(2)}) %collective-permute-start.9) | collective-permute-done | bytes 16416 | tf_op jit(solution)/shard_map/ppermute | solution.py:13
  66.4 0.0 collective-permute-start.10
  66.4 0.7 compare_select_fusion
  67.0 5.2 %collective-permute-done.10 = bf16[64,1,128]{2,0,1:T(8,128)(2,1)S(1)} collective-permute-done((bf16[64,1,128]{2,0,1:T(8,128)(2,1)S(1)}, bf16[64,1,128]{2,0,1:T(8,128)(2,1)S(1)}, u32[]{:S(2)}, u32[]{:S(2)}) %collective-permute-start.10) | collective-permute-done | bytes 16416 | tf_op jit(solution)/shard_map/ppermute | solution.py:13
  72.2 0.0 collective-permute-start.11
  72.3 0.6 gather_fusion
  72.9 5.2 %collective-permute-done.11 = bf16[64,1,128]{2,0,1:T(8,128)(2,1)S(1)} collective-permute-done((bf16[64,1,128]{2,0,1:T(8,128)(2,1)S(1)}, bf16[64,1,128]{2,0,1:T(8,128)(2,1)S(1)}, u32[]{:S(2)}, u32[]{:S(2)}) %collective-permute-start.11) | collective-permute-done | bytes 16416 | tf_op jit(solution)/shard_map/ppermute | solution.py:13
  78.1 0.0 collective-permute-start.12
  78.1 5.8 %collective-permute-done.12 = bf16[64,1,128]{2,0,1:T(8,128)(2,1)S(1)} collective-permute-done((bf16[64,1,128]{2,0,1:T(8,128)(2,1)S(1)}, bf16[64,1,128]{2,0,1:T(8,128)(2,1)S(1)}, u32[]{:S(2)}, u32[]{:S(2)}) %collective-permute-start.12) | collective-permute-done | bytes 16416 | tf_op jit(solution)/shard_map/ppermute | solution.py:13
  84.0 0.0 collective-permute-start.13
  84.0 0.1 add_compare_fusion
  84.0 5.8 %collective-permute-done.13 = bf16[64,1,128]{2,0,1:T(8,128)(2,1)S(1)} collective-permute-done((bf16[64,1,128]{2,0,1:T(8,128)(2,1)S(1)}, bf16[64,1,128]{2,0,1:T(8,128)(2,1)S(1)}, u32[]{:S(2)}, u32[]{:S(2)}) %collective-permute-start.13) | collective-permute-done | bytes 16416 | tf_op jit(solution)/shard_map/ppermute | solution.py:13
  89.8 0.1 iota_compare_fusion
  89.9 5.8 %collective-permute-done.14 = bf16[64,1,128]{2,0,1:T(8,128)(2,1)S(1)} collective-permute-done((bf16[64,1,128]{2,0,1:T(8,128)(2,1)S(1)}, bf16[64,1,128]{2,0,1:T(8,128)(2,1)S(1)}, u32[]{:S(2)}, u32[]{:S(2)}) %collective-permute-start.14) | collective-permute-done | bytes 16416 | tf_op jit(solution)/shard_map/ppermute | solution.py:13
  95.9 0.7 constant_dynamic-update-slice_fusion.16
  96.8 0.7 constant_dynamic-update-slice_fusion
  97.5 0.6 gather_fusion.1
  98.1 5.8 %select_reduce_fusion = (f32[8,8,8]{2,1,0:T(8,128)S(1)}, f32[8,8,8,512]{3,2,1,0:T(8,128)S(1)}) fusion(pred[8,512]{1,0:T(8,128)(4,1)S(1)} %add_compare_fusion, bf16[8,512,8,128]{3,2,1,0:T(8,128)(2,1)} %param.6, bf16[8,8,8,128]{3,2,1,0:T(8,128)(2,1)S(1)} %gather_fusion.1, pred[8]{0:T(512)(128)(4,1)S(1)} %get-tuple-element.8), kind=kOutput, calls=%fused_computation.14 | convolution fusion | flops 67960320 | bytes 9574408 | tf_op jit(solution)/shard_map/vmap(kgd,tkd->kgt)/dot_general | solution.py:21
  103.9 0.1 select_reduce_fusion.1
  104.0 57.6 %pmax.7 = f32[16,8,8]{0,2,1:T(8,128)S(1)} all-reduce(f32[16,8,8]{0,2,1:T(8,128)S(1)} %select_reduce_fusion.1), channel_id=1, replica_groups=mesh['grp'=2,'seq'=16,'head'=1] {'seq'}, use_global_device_ids=true, to_apply=%region_2.3 | all-reduce | flops 1024 | bytes 8192 | tf_op jit(solution)/shard_map/pmax | solution.py:58
  161.7 0.1 copy.23
  161.8 0.6 gather_fusion.2
  162.3 0.4 convert_reduce_fusion
  162.7 0.1 fusion.23
  162.8 5.0 %fusion.7 = f32[8,8,8,128]{3,2,1,0:T(8,128)S(1)} fusion(bf16[8,512,8,128]{3,2,1,0:T(8,128)(2,1)} %param.7, f32[8,8,8]{2,1,0:T(8,128)S(1)} %get-tuple-element.6, f32[8,8,8,512]{3,2,1,0:T(8,128)S(1)} %get-tuple-element.13, f32[8,8,8]{2,1,0:T(8,128)S(1)} %get-tuple-element.12, pred[8,512]{1,0:T(8,128)(4,1)S(1)} %add_compare_fusion), kind=kOutput, calls=%fused_computation.9 | convolution fusion | flops 67960832 | bytes 9707520 | tf_op jit(solution)/shard_map/vmap(kgt,tkd->kgd)/dot_general | solution.py:26
  167.8 0.6 convolution_multiply_fusion
  168.3 1.0 copy.26
  169.3 0.0 reduce-scatter.2.cloned.1.call-update
  169.3 0.6 dynamic-slice
  170.6 0.1 copy.27
  170.6 0.2 fusion.10
  170.9 0.1 copy.28
  170.9 0.1 reshape.84
  171.0 29.6 %all-reduce = f32[1024]{0:T(1024)S(1)} all-reduce(f32[1024]{0:T(1024)S(1)} %reshape.84), channel_id=3, replica_groups=mesh['grp'=2,'seq'=16,'head'=1] {'seq'}, use_global_device_ids=true, to_apply=%region_5.6.clone | all-reduce | flops 1024 | bytes 8192
  200.6 0.1 dynamic-slice.1
  200.7 22.7 %reduce-scatter.2.cloned.1.call-done = f32[64,128]{1,0:T(8,128)} async-done(((f32[1024,128]{1,0:T(8,128)}), f32[64,128]{1,0:T(8,128)}) %reduce-scatter.2.cloned.1.call-update) | async-done | bytes 32784 | tf_op jit(solution)/shard_map/reduce_scatter | solution.py:64
  223.4 1.4 fusion.16
  (48 shorter events, 0.3 us)
Async XLA Ops:
  6.5 65.7 %copy-start = (s32[16]{0:T(128)S(1)}, s32[16]{0:T(128)}, u32[]{:S(2)}) copy-start(s32[16]{0:T(128)} %param.8) | copy-start | bytes 196
  6.5 216.9 %reduce-scatter.2.cloned.1.call-start = ((), (), s32[]{:S(2)}) async-start(), calls=%async_computation.1 | async-start | bytes 557056 | tf_op jit(solution)/shard_map/reduce_scatter | solution.py:64
  6.5 7.1 %collective-permute-start = (bf16[64,1,128]{2,0,1:T(8,128)(2,1)}, bf16[64,1,128]{2,0,1:T(8,128)(2,1)S(1)}, u32[]{:S(2)}, u32[]{:S(2)}) collective-permute-start(bf16[64,1,128]{2,0,1:T(8,128)(2,1)} %param.5), channel_id=1, source_target_pairs={{0,1},{1,2},{2,3},{3,4},{4,5},{5,6},{6,7},{7,8},{8,9},{9,10},{10,1... | collective-permute-start | bytes 49160 | tf_op jit(solution)/shard_map/ppermute | solution.py:13
  13.6 5.9 %collective-permute-start.1 = (bf16[64,1,128]{2,0,1:T(8,128)(2,1)S(1)}, bf16[64,1,128]{2,0,1:T(8,128)(2,1)S(1)}, u32[]{:S(2)}, u32[]{:S(2)}) collective-permute-start(bf16[64,1,128]{2,0,1:T(8,128)(2,1)S(1)} %collective-permute-done), channel_id=1, source_target_pairs={{0,1},{1,2},{2,3},{3,4},{4,5},{5,6},{6,7},{7,8},{8,9},{9,10},{10,1... | collective-permute-start | bytes 49160 | tf_op jit(solution)/shard_map/ppermute | solution.py:13
  19.5 5.9 %collective-permute-start.2 = (bf16[64,1,128]{2,0,1:T(8,128)(2,1)S(1)}, bf16[64,1,128]{2,0,1:T(8,128)(2,1)S(1)}, u32[]{:S(2)}, u32[]{:S(2)}) collective-permute-start(bf16[64,1,128]{2,0,1:T(8,128)(2,1)S(1)} %collective-permute-done.1), channel_id=1, source_target_pairs={{0,1},{1,2},{2,3},{3,4},{4,5},{5,6},{6,7},{7,8},{8,9},{9,10},{10,1... | collective-permute-start | bytes 49160 | tf_op jit(solution)/shard_map/ppermute | solution.py:13
  25.3 5.9 %collective-permute-start.3 = (bf16[64,1,128]{2,0,1:T(8,128)(2,1)S(1)}, bf16[64,1,128]{2,0,1:T(8,128)(2,1)S(1)}, u32[]{:S(2)}, u32[]{:S(2)}) collective-permute-start(bf16[64,1,128]{2,0,1:T(8,128)(2,1)S(1)} %collective-permute-done.2), channel_id=1, source_target_pairs={{0,1},{1,2},{2,3},{3,4},{4,5},{5,6},{6,7},{7,8},{8,9},{9,10},{10,1... | collective-permute-start | bytes 49160 | tf_op jit(solution)/shard_map/ppermute | solution.py:13
  31.2 5.9 %collective-permute-start.4 = (bf16[64,1,128]{2,0,1:T(8,128)(2,1)S(1)}, bf16[64,1,128]{2,0,1:T(8,128)(2,1)S(1)}, u32[]{:S(2)}, u32[]{:S(2)}) collective-permute-start(bf16[64,1,128]{2,0,1:T(8,128)(2,1)S(1)} %collective-permute-done.3), channel_id=1, source_target_pairs={{0,1},{1,2},{2,3},{3,4},{4,5},{5,6},{6,7},{7,8},{8,9},{9,10},{10,1... | collective-permute-start | bytes 49160 | tf_op jit(solution)/shard_map/ppermute | solution.py:13
  37.1 5.9 %collective-permute-start.5 = (bf16[64,1,128]{2,0,1:T(8,128)(2,1)S(1)}, bf16[64,1,128]{2,0,1:T(8,128)(2,1)S(1)}, u32[]{:S(2)}, u32[]{:S(2)}) collective-permute-start(bf16[64,1,128]{2,0,1:T(8,128)(2,1)S(1)} %collective-permute-done.4), channel_id=1, source_target_pairs={{0,1},{1,2},{2,3},{3,4},{4,5},{5,6},{6,7},{7,8},{8,9},{9,10},{10,1... | collective-permute-start | bytes 49160 | tf_op jit(solution)/shard_map/ppermute | solution.py:13
  42.9 5.9 %collective-permute-start.6 = (bf16[64,1,128]{2,0,1:T(8,128)(2,1)S(1)}, bf16[64,1,128]{2,0,1:T(8,128)(2,1)S(1)}, u32[]{:S(2)}, u32[]{:S(2)}) collective-permute-start(bf16[64,1,128]{2,0,1:T(8,128)(2,1)S(1)} %collective-permute-done.5), channel_id=1, source_target_pairs={{0,1},{1,2},{2,3},{3,4},{4,5},{5,6},{6,7},{7,8},{8,9},{9,10},{10,1... | collective-permute-start | bytes 49160 | tf_op jit(solution)/shard_map/ppermute | solution.py:13
  48.8 5.9 %collective-permute-start.7 = (bf16[64,1,128]{2,0,1:T(8,128)(2,1)S(1)}, bf16[64,1,128]{2,0,1:T(8,128)(2,1)S(1)}, u32[]{:S(2)}, u32[]{:S(2)}) collective-permute-start(bf16[64,1,128]{2,0,1:T(8,128)(2,1)S(1)} %collective-permute-done.6), channel_id=1, source_target_pairs={{0,1},{1,2},{2,3},{3,4},{4,5},{5,6},{6,7},{7,8},{8,9},{9,10},{10,1... | collective-permute-start | bytes 49160 | tf_op jit(solution)/shard_map/ppermute | solution.py:13
  54.6 5.9 %collective-permute-start.8 = (bf16[64,1,128]{2,0,1:T(8,128)(2,1)S(1)}, bf16[64,1,128]{2,0,1:T(8,128)(2,1)S(1)}, u32[]{:S(2)}, u32[]{:S(2)}) collective-permute-start(bf16[64,1,128]{2,0,1:T(8,128)(2,1)S(1)} %collective-permute-done.7), channel_id=1, source_target_pairs={{0,1},{1,2},{2,3},{3,4},{4,5},{5,6},{6,7},{7,8},{8,9},{9,10},{10,1... | collective-permute-start | bytes 49160 | tf_op jit(solution)/shard_map/ppermute | solution.py:13
  60.5 5.9 %collective-permute-start.9 = (bf16[64,1,128]{2,0,1:T(8,128)(2,1)S(1)}, bf16[64,1,128]{2,0,1:T(8,128)(2,1)S(1)}, u32[]{:S(2)}, u32[]{:S(2)}) collective-permute-start(bf16[64,1,128]{2,0,1:T(8,128)(2,1)S(1)} %collective-permute-done.8), channel_id=1, source_target_pairs={{0,1},{1,2},{2,3},{3,4},{4,5},{5,6},{6,7},{7,8},{8,9},{9,10},{10,1... | collective-permute-start | bytes 49160 | tf_op jit(solution)/shard_map/ppermute | solution.py:13
  66.4 5.9 %collective-permute-start.10 = (bf16[64,1,128]{2,0,1:T(8,128)(2,1)S(1)}, bf16[64,1,128]{2,0,1:T(8,128)(2,1)S(1)}, u32[]{:S(2)}, u32[]{:S(2)}) collective-permute-start(bf16[64,1,128]{2,0,1:T(8,128)(2,1)S(1)} %collective-permute-done.9), channel_id=1, source_target_pairs={{0,1},{1,2},{2,3},{3,4},{4,5},{5,6},{6,7},{7,8},{8,9},{9,10},{10,1... | collective-permute-start | bytes 49160 | tf_op jit(solution)/shard_map/ppermute | solution.py:13
  72.2 5.9 %collective-permute-start.11 = (bf16[64,1,128]{2,0,1:T(8,128)(2,1)S(1)}, bf16[64,1,128]{2,0,1:T(8,128)(2,1)S(1)}, u32[]{:S(2)}, u32[]{:S(2)}) collective-permute-start(bf16[64,1,128]{2,0,1:T(8,128)(2,1)S(1)} %collective-permute-done.10), channel_id=1, source_target_pairs={{0,1},{1,2},{2,3},{3,4},{4,5},{5,6},{6,7},{7,8},{8,9},{9,10},{10,1... | collective-permute-start | bytes 49160 | tf_op jit(solution)/shard_map/ppermute | solution.py:13
  78.1 5.9 %collective-permute-start.12 = (bf16[64,1,128]{2,0,1:T(8,128)(2,1)S(1)}, bf16[64,1,128]{2,0,1:T(8,128)(2,1)S(1)}, u32[]{:S(2)}, u32[]{:S(2)}) collective-permute-start(bf16[64,1,128]{2,0,1:T(8,128)(2,1)S(1)} %collective-permute-done.11), channel_id=1, source_target_pairs={{0,1},{1,2},{2,3},{3,4},{4,5},{5,6},{6,7},{7,8},{8,9},{9,10},{10,1... | collective-permute-start | bytes 49160 | tf_op jit(solution)/shard_map/ppermute | solution.py:13
  84.0 5.9 %collective-permute-start.13 = (bf16[64,1,128]{2,0,1:T(8,128)(2,1)S(1)}, bf16[64,1,128]{2,0,1:T(8,128)(2,1)S(1)}, u32[]{:S(2)}, u32[]{:S(2)}) collective-permute-start(bf16[64,1,128]{2,0,1:T(8,128)(2,1)S(1)} %collective-permute-done.12), channel_id=1, source_target_pairs={{0,1},{1,2},{2,3},{3,4},{4,5},{5,6},{6,7},{7,8},{8,9},{9,10},{10,1... | collective-permute-start | bytes 49160 | tf_op jit(solution)/shard_map/ppermute | solution.py:13
  89.8 5.9 %collective-permute-start.14 = (bf16[64,1,128]{2,0,1:T(8,128)(2,1)S(1)}, bf16[64,1,128]{2,0,1:T(8,128)(2,1)S(1)}, u32[]{:S(2)}, u32[]{:S(2)}) collective-permute-start(bf16[64,1,128]{2,0,1:T(8,128)(2,1)S(1)} %collective-permute-done.13), channel_id=1, source_target_pairs={{0,1},{1,2},{2,3},{3,4},{4,5},{5,6},{6,7},{7,8},{8,9},{9,10},{10,1... | collective-permute-start | bytes 49160 | tf_op jit(solution)/shard_map/ppermute | solution.py:13
  103.9 65.4 %copy-start.1 = (u32[32]{0:T(128)S(1)}, u32[32]{0:T(128)}, u32[]{:S(2)}) copy-start(u32[32]{0:T(128)} %constant.112) | copy-start | bytes 388
Sparse Core Ops, SparseCore 0:
  169.4 53.9 reduce-scatter.1
